TPU v7x, 32 devices: a whole 2x2x4 slice. The times are simulated.
32 devices in a mesh: north: 4 (over y, x), east: 8 (over z, core).
Axes of the slice: x: 2, y: 2, z: 4, core: 2. Of those that a mesh axis runs over, the one named last changes fastest.
Arguments:
- pair_rows: bfloat16 [96, 96, 128], P('north', 'east'), may hold values from -6 to 6
- in_gain: float32 [128], replicated, may hold values from 0.25 to 1.75
- left_weight: bfloat16 [128, 128], replicated, may hold values from -0.5 to 0.5
- right_weight: bfloat16 [128, 128], replicated, may hold values from -0.5 to 0.5
- left_gate: bfloat16 [128, 128], replicated, may hold values from -0.5 to 0.5
- right_gate: bfloat16 [128, 128], replicated, may hold values from -0.5 to 0.5
- mid_gain: float32 [128], replicated, may hold values from 0.25 to 1.75
- out_weight: bfloat16 [128, 128], replicated, may hold values from -0.5 to 0.5
- out_gate: bfloat16 [128, 128], replicated, may hold values from -0.5 to 0.5
Outputs:
- pair_change: bfloat16 [96, 96, 128], P('north', 'east')
All inputs are finite; a program needn't handle non-finite values.
Results may differ from a plain program's by a relative error of at most 0.012.
Values may be sent and summed in bfloat16 or wider, within the bound.
A program may use at most 128 MiB of HBM per device.

v0:
```python
import jax
import jax.numpy as jnp
from jax import lax
from jax.sharding import PartitionSpec as P


def scale_channels(values, channel_gain):
    centred = values - jnp.mean(values, axis=-1, keepdims=True)
    return (
        centred
        * lax.rsqrt(jnp.mean(centred * centred, axis=-1, keepdims=True) + 1e-05)
        * channel_gain
    )


def both_factors(pair_in, in_gain, left_weight, right_weight, left_gate, right_gate):
    ready = scale_channels(pair_in.astype(jnp.float32), in_gain).astype(jnp.bfloat16)
    ready = lax.optimization_barrier(ready)
    left = jnp.einsum("ijc,cd->ijd", ready, left_weight, preferred_element_type=jnp.float32)
    left = left * jax.nn.sigmoid(
        jnp.einsum("ijc,cd->ijd", ready, left_gate, preferred_element_type=jnp.float32)
    )
    right = jnp.einsum("ijc,cd->ijd", ready, right_weight, preferred_element_type=jnp.float32)
    right = right * jax.nn.sigmoid(
        jnp.einsum("ijc,cd->ijd", ready, right_gate, preferred_element_type=jnp.float32)
    )
    return (ready, left.astype(jnp.bfloat16), right.astype(jnp.bfloat16))


def to_pair(mixed, ready, mid_gain, out_weight, out_gate):
    scaled = scale_channels(mixed.astype(jnp.float32), mid_gain).astype(jnp.bfloat16)
    scaled = lax.optimization_barrier(scaled)
    gate = jax.nn.sigmoid(
        jnp.einsum("ijc,cd->ijd", ready, out_gate, preferred_element_type=jnp.float32)
    )
    return (
        jnp.einsum("ijd,dc->ijc", scaled, out_weight, preferred_element_type=jnp.float32) * gate
    ).astype(jnp.bfloat16)


def body(
    pair_rows,
    in_gain,
    left_weight,
    right_weight,
    left_gate,
    right_gate,
    mid_gain,
    out_weight,
    out_gate,
):
    ready, left, right = both_factors(
        pair_rows, in_gain, left_weight, right_weight, left_gate, right_gate
    )
    count = pair_rows.shape[0] * lax.axis_size("north")
    left_lines, right_lines = (
        lax.all_to_all(left, "north", split_axis=2, concat_axis=0, tiled=True),
        lax.all_to_all(right, "north", split_axis=2, concat_axis=0, tiled=True),
    )
    strip = jnp.einsum(
        "kid,kjd->ijd",
        lax.all_gather(left_lines, "east", axis=1, tiled=True),
        right_lines,
        preferred_element_type=jnp.float32,
    )
    strip = (strip * count ** (-0.5)).astype(jnp.bfloat16)
    mixed = lax.all_to_all(strip, "north", split_axis=0, concat_axis=2, tiled=True)
    return to_pair(mixed, ready, mid_gain, out_weight, out_gate)


def solution(mesh):
    placed = (P("north", "east", None), P(), P(), P(), P(), P(), P(), P(), P())
    return jax.shard_map(
        body, mesh=mesh, in_specs=placed, out_specs=P("north", "east", None), check_vma=False
    )
```

profile of v0, /device:TPU:0, one launch (start us, length us, event | category | flops | bytes accessed | tf_op | source)
XLA Modules:
  0.0 53.7 jit_solution(4240854814656932525)
XLA Ops:
  0.0 0.0 copy-start
  0.0 0.0 copy-start.1
  0.0 1.1 %convert_reduce_fusion = f32[24,12]{0,1:T(8,128)S(1)} fusion(bf16[24,12,128]{2,0,1:T(8,128)(2,1)} %param.9), kind=kLoop, calls=%fused_computation.26 | loop fusion | flops 73440 | bytes 74880 | tf_op jit(solution)/shard_map/reduce_sum | solution.py:8
  1.1 0.0 copy-done.1
  1.1 0.2 fusion.20
  1.3 0.0 copy-start.4
  1.3 0.6 %copy-done.4 = f32[128]{0:T(128)S(1)} copy-done((f32[128]{0:T(128)S(1)}, f32[128]{0:T(128)}, u32[]{:S(2)}) %copy-start.4) | copy-done | bytes 536
  2.0 0.1 fusion.22
  2.1 0.0 copy-done
  2.1 0.0 copy-start.6
  2.1 0.2 fusion.31
  2.3 0.6 %copy-done.6 = bf16[128,128]{1,0:T(8,128)(2,1)S(1)} copy-done((bf16[128,128]{1,0:T(8,128)(2,1)S(1)}, bf16[128,128]{1,0:T(8,128)(2,1)}, u32[]{:S(2)}) %copy-start.6) | copy-done | bytes 32792
  2.9 0.2 fusion.16
  3.1 0.4 copy.42
  3.5 1.1 %reshape.43 = bf16[4,2,4608]{2,1,0:T(2,128)(2,1)} reshape(bf16[128,12,24]{2,1,0:T(8,128)(2,1)S(1)} %bitcast.52) | data formatting | bytes 147456
  4.6 0.0 copy-start.2
  4.6 5.3 %all-to-all-start = ((bf16[4,2,4608]{2,1,0:T(2,128)(2,1)}), bf16[4,2,4608]{2,1,0:T(2,128)(2,1)S(1)}, u32[]{:S(2)}, u32[]{:S(2)}) async-start(bf16[4,2,4608]{2,1,0:T(2,128)(2,1)} %reshape.43), calls=%async_computation | async-start | bytes 147456 | tf_op jit(solution)/shard_map/all_to_all | solution.py:58
  10.0 0.0 copy-done.2
  10.0 0.0 copy-start.7
  10.0 0.2 fusion.28
  10.1 0.6 %copy-done.7 = bf16[128,128]{1,0:T(8,128)(2,1)S(1)} copy-done((bf16[128,128]{1,0:T(8,128)(2,1)S(1)}, bf16[128,128]{1,0:T(8,128)(2,1)}, u32[]{:S(2)}) %copy-start.7) | copy-done | bytes 32792
  10.7 0.2 fusion.15
  10.9 0.4 copy.44
  11.4 1.1 %reshape.41 = bf16[4,2,4608]{2,1,0:T(2,128)(2,1)} reshape(bf16[128,12,24]{2,1,0:T(8,128)(2,1)S(1)} %bitcast.53) | data formatting | bytes 147456
  12.5 2.3 %all-to-all-done = bf16[4,2,4608]{2,1,0:T(2,128)(2,1)S(1)} async-done(((bf16[4,2,4608]{2,1,0:T(2,128)(2,1)}), bf16[4,2,4608]{2,1,0:T(2,128)(2,1)S(1)}, u32[]{:S(2)}, u32[]{:S(2)}) %all-to-all-start) | async-done | bytes 73760 | tf_op jit(solution)/shard_map/all_to_all | solution.py:58
  14.8 3.3 %all-to-all-start.1 = ((bf16[4,2,4608]{2,1,0:T(2,128)(2,1)}), bf16[4,2,4608]{2,1,0:T(2,128)(2,1)S(1)}, u32[]{:S(2)}, u32[]{:S(2)}) async-start(bf16[4,2,4608]{2,1,0:T(2,128)(2,1)} %reshape.41), calls=%async_computation.1 | async-start | bytes 147456 | tf_op jit(solution)/shard_map/all_to_all | solution.py:57
  18.1 0.6 %reshape.44 = bf16[128,12,24]{2,1,0:T(8,128)(2,1)S(1)} reshape(bf16[4,2,4608]{2,1,0:T(2,128)(2,1)S(1)} %all-to-all-done) | data formatting | bytes 147456
  18.7 0.3 copy.58
  19.1 0.2 all_to_all.36
  19.3 3.7 %all-to-all-done.1 = bf16[4,2,4608]{2,1,0:T(2,128)(2,1)S(1)} async-done(((bf16[4,2,4608]{2,1,0:T(2,128)(2,1)}), bf16[4,2,4608]{2,1,0:T(2,128)(2,1)S(1)}, u32[]{:S(2)}, u32[]{:S(2)}) %all-to-all-start.1) | async-done | bytes 73760 | tf_op jit(solution)/shard_map/all_to_all | solution.py:57
  23.0 0.6 %reshape.42 = bf16[128,12,24]{2,1,0:T(8,128)(2,1)S(1)} reshape(bf16[4,2,4608]{2,1,0:T(2,128)(2,1)S(1)} %all-to-all-done.1) | data formatting | bytes 147456
  23.6 0.3 copy.57
  23.9 0.2 all_to_all.40
  24.1 16.5 %all_gather.3 = bf16[96,96,32]{0,2,1:T(8,128)(2,1)S(1)} all-gather(bf16[96,12,32]{0,2,1:T(8,128)(2,1)S(1)} %all_to_all.40), channel_id=1, replica_groups=mesh['north'=4,'east'=8] {'east'}, dimensions={1}, use_global_device_ids=true | all-gather | bytes 663552 | tf_op jit(solution)/shard_map/all_gather | solution.py:62
  40.6 0.5 fusion.13
  41.1 0.4 copy.48
  41.5 0.3 reshape.45
  41.8 7.2 %all_to_all.45 = bf16[4,2,4608]{2,1,0:T(2,128)(2,1)S(1)} all-to-all(bf16[4,2,4608]{2,1,0:T(2,128)(2,1)S(1)} %reshape.45), channel_id=1, replica_groups=mesh['north'=4,'east'=8] {'north'}, dimensions={0} | all-to-all | bytes 147456 | tf_op jit(solution)/shard_map/all_to_all | solution.py:67
  49.1 0.2 reshape.46
  49.3 0.3 copy.49
  49.6 0.4 reshape.34
  50.0 0.1 bitcast_reduce_fusion
  50.1 0.3 multiply_reduce_fusion
  50.4 0.3 copy.50
  50.7 0.0 copy-start.5
  50.7 0.3 reshape.32
  51.0 0.4 copy-done.5
  51.4 0.0 copy-start.3
  51.4 0.1 multiply_convert_fusion
  51.5 0.6 %copy-done.3 = bf16[128,128]{1,0:T(8,128)(2,1)S(1)} copy-done((bf16[128,128]{1,0:T(8,128)(2,1)S(1)}, bf16[128,128]{1,0:T(8,128)(2,1)}, u32[]{:S(2)}) %copy-start.3) | copy-done | bytes 32792
  52.1 0.0 copy-start.8
  52.1 0.2 fusion.25
  52.3 0.6 %copy-done.8 = bf16[128,128]{1,0:T(8,128)(2,1)S(1)} copy-done((bf16[128,128]{1,0:T(8,128)(2,1)S(1)}, bf16[128,128]{1,0:T(8,128)(2,1)}, u32[]{:S(2)}) %copy-start.8) | copy-done | bytes 32792
  52.9 0.8 %fusion.14 = bf16[24,12,128]{2,0,1:T(8,128)(2,1)} fusion(f32[24,12,128]{2,0,1:T(8,128)S(1)} %fusion.25, bf16[24,12,128]{2,0,1:T(8,128)(2,1)S(1)} %fusion.22, bf16[128,128]{1,0:T(8,128)(2,1)S(1)} %copy-done.8), kind=kOutput, calls=%fused_computation.18 | convolution fusion | flops 9621504 | bytes 327680 | tf_op jit(solution)/shard_map/ijc,cd->ijd/dot_general | solution.py:34
  (4 shorter events, 0.0 us)
Async XLA Ops:
  0.0 2.1 %copy-start = (bf16[128,128]{1,0:T(8,128)(2,1)S(1)}, bf16[128,128]{1,0:T(8,128)(2,1)}, u32[]{:S(2)}) copy-start(bf16[128,128]{1,0:T(8,128)(2,1)} %param.12) | copy-start | bytes 98308
  0.0 1.1 %copy-start.1 = (bf16[24,12,128]{2,0,1:T(8,128)(2,1)S(1)}, bf16[24,12,128]{2,0,1:T(8,128)(2,1)}, u32[]{:S(2)}) copy-start(bf16[24,12,128]{2,0,1:T(8,128)(2,1)} %param.9) | copy-start | bytes 221188
  1.3 0.7 %copy-start.4 = (f32[128]{0:T(128)S(1)}, f32[128]{0:T(128)}, u32[]{:S(2)}) copy-start(f32[128]{0:T(128)} %param.10) | copy-start | bytes 1540
  2.1 0.8 %copy-start.6 = (bf16[128,128]{1,0:T(8,128)(2,1)S(1)}, bf16[128,128]{1,0:T(8,128)(2,1)}, u32[]{:S(2)}) copy-start(bf16[128,128]{1,0:T(8,128)(2,1)} %param.14) | copy-start | bytes 98308
  4.6 5.3 %copy-start.2 = (bf16[128,128]{1,0:T(8,128)(2,1)S(1)}, bf16[128,128]{1,0:T(8,128)(2,1)}, u32[]{:S(2)}) copy-start(bf16[128,128]{1,0:T(8,128)(2,1)} %param.11) | copy-start | bytes 98308
  4.6 10.2 %all-to-all-start = ((bf16[4,2,4608]{2,1,0:T(2,128)(2,1)}), bf16[4,2,4608]{2,1,0:T(2,128)(2,1)S(1)}, u32[]{:S(2)}, u32[]{:S(2)}) async-start(bf16[4,2,4608]{2,1,0:T(2,128)(2,1)} %reshape.43), calls=%async_computation | async-start | bytes 147456 | tf_op jit(solution)/shard_map/all_to_all | solution.py:58
  10.0 0.8 %copy-start.7 = (bf16[128,128]{1,0:T(8,128)(2,1)S(1)}, bf16[128,128]{1,0:T(8,128)(2,1)}, u32[]{:S(2)}) copy-start(bf16[128,128]{1,0:T(8,128)(2,1)} %param.13) | copy-start | bytes 98308
  14.8 8.1 %all-to-all-start.1 = ((bf16[4,2,4608]{2,1,0:T(2,128)(2,1)}), bf16[4,2,4608]{2,1,0:T(2,128)(2,1)S(1)}, u32[]{:S(2)}, u32[]{:S(2)}) async-start(bf16[4,2,4608]{2,1,0:T(2,128)(2,1)} %reshape.41), calls=%async_computation.1 | async-start | bytes 147456 | tf_op jit(solution)/shard_map/all_to_all | solution.py:57
  50.7 0.7 %copy-start.5 = (f32[128]{0:T(128)S(1)}, f32[128]{0:T(128)}, u32[]{:S(2)}) copy-start(f32[128]{0:T(128)} %param.15) | copy-start | bytes 1540
  51.4 0.8 %copy-start.3 = (bf16[128,128]{1,0:T(8,128)(2,1)S(1)}, bf16[128,128]{1,0:T(8,128)(2,1)}, u32[]{:S(2)}) copy-start(bf16[128,128]{1,0:T(8,128)(2,1)} %param.16) | copy-start | bytes 98308
  52.1 0.8 %copy-start.8 = (bf16[128,128]{1,0:T(8,128)(2,1)S(1)}, bf16[128,128]{1,0:T(8,128)(2,1)}, u32[]{:S(2)}) copy-start(bf16[128,128]{1,0:T(8,128)(2,1)} %param.17) | copy-start | bytes 98308
where the time goes:
time: 54.5 us; the launch traced here: 53.7 us
  blocking collectives  23.7 us (43%)
  local copies, waits for them, and re-layouts  11 us (20%)
  starting transfers between devices  8.61 us (16%)
  waiting for transfers between devices  6 us (11%)
  matrix products  2.22 us (4%)
  other arithmetic  1.94 us (4%)
    all_gather x1, blocking collectives, body(): lax.all_gather(left_lines, 'east', axis=1, tiled=True)  16.5 us
    unnamed x24, local copies, waits for them, and re-layouts  7.43 us
    all_to_all x1, blocking collectives, body(): lax.all_to_all(strip, 'north', split_axis=0, concat_axis=2, tiled=True)  7.23 us
    all_to_all x1, starting transfers between devices, body(): lax.all_to_all(right, 'north', split_axis=2, concat_axis=0, tiled=True)  5.32 us
    all_to_all x1, waiting for transfers between devices, body(): lax.all_to_all(left, 'north', split_axis=2, concat_axis=0, tiled=True)  3.68 us
    all_to_all x1, starting transfers between devices, body(): lax.all_to_all(left, 'north', split_axis=2, concat_axis=0, tiled=True)  3.29 us
    all_to_all x1, waiting for transfers between devices, body(): lax.all_to_all(right, 'north', split_axis=2, concat_axis=0, tiled=True)  2.32 us
    reduce_sum x2, other arithmetic, scale_channels(): centred = values - jnp.mean(values, axis=-1, keepdims=True)  1.18 us
  transfers between devices with their start and end apart: 2, of which 2 were waited for; matrix products, arithmetic and copies ran while one was open for 5% of the time, Pallas kernels for 0%

commit v1 on v0

v1 whole, which is shorter than its diff:
```python
import functools

import jax
import jax.numpy as jnp
from jax import lax
from jax.experimental import pallas as pl
from jax.experimental.pallas import tpu as pltpu
from jax.sharding import PartitionSpec as P

MESH = pl.DeviceIdType.MESH
F32 = jnp.float32
BF16 = jnp.bfloat16
LANES = 8


def scale_channels(values, channel_gain):
    centred = values - jnp.mean(values, axis=-1, keepdims=True)
    return (
        centred
        * lax.rsqrt(jnp.mean(centred * centred, axis=-1, keepdims=True) + 1e-05)
        * channel_gain
    )


def nearest_first(chips):
    return [sorted(range(chips), key=lambda other: (abs(other - z), other)) for z in range(chips)]


def kernel(
    norths,
    easts,
    lines,
    columns,
    pair_hbm,
    in_gain_hbm,
    left_weight_hbm,
    right_weight_hbm,
    left_gate_hbm,
    right_gate_hbm,
    mid_gain_hbm,
    out_weight_hbm,
    out_gate_hbm,
    out_ref,
    pair_in,
    gains,
    weights,
    rows32,
    ready_ref,
    gate_ref,
    left_all,
    left32,
    right_own,
    right_partner,
    right32,
    sums32,
    sums_dense,
    sums_send,
    sums_all,
    load_sem,
    left_send_sem,
    left_recv_sem,
    right_sem,
    sums_send_sem,
    sums_recv_sem,
):
    rows, width = pair_in.shape
    chips = easts // 2
    ratio = lines // columns
    piece = columns * columns

    north = lax.axis_index("north")
    east = lax.axis_index("east")
    chip = east // 2
    core = east % 2
    partner = chip * 2 + 1 - core

    loads = [
        (pair_hbm, pair_in),
        (in_gain_hbm, gains.at[pl.ds(0, 1)]),
        (left_weight_hbm, weights.at[0]),
        (left_gate_hbm, weights.at[1]),
        (right_weight_hbm, weights.at[2]),
        (right_gate_hbm, weights.at[3]),
        (out_gate_hbm, weights.at[4]),
        (out_weight_hbm, weights.at[5]),
        (mid_gain_hbm, gains.at[pl.ds(8, 1)]),
    ]
    loads = [
        pltpu.make_async_copy(source, target, load_sem.at[at])
        for at, (source, target) in enumerate(loads)
    ]
    for load in loads:
        load.start()

    barrier = pltpu.get_barrier_semaphore()
    for step in range(1, chips):
        there = lax.rem(chip + step, chips)
        pl.semaphore_signal(
            barrier, inc=1, device_id=(north, there * 2 + core), device_id_type=MESH
        )
    for step in range(norths):
        there = lax.rem(north + step, norths)
        if step:
            pl.semaphore_signal(barrier, inc=1, device_id=(there, east), device_id_type=MESH)
        pl.semaphore_signal(barrier, inc=1, device_id=(there, partner), device_id_type=MESH)

    table = nearest_first(chips)
    order = []
    for step in range(1, chips):
        other = jnp.int32(0)
        for z in range(chips):
            other = other + (chip == z).astype(jnp.int32) * table[z][step]
        order.append(other)

    loads[0].wait()
    loads[1].wait()

    chunk = rows // max(1, rows // 288)
    if rows % chunk or chunk % 16:
        chunk = rows

    def in_chunks(step):
        if chunk == rows:
            step(pl.ds(0, rows))
        else:

            @pl.loop(0, rows // chunk)
            def _(at):
                step(pl.ds(pl.multiple_of(at * chunk, chunk), chunk))

    def project(ready, which):
        return jnp.dot(ready, weights[which], preferred_element_type=F32)

    loads[2].wait()
    loads[3].wait()

    def left_chunk(part):
        ready = scale_channels(pair_in[part, :].astype(F32), gains[pl.ds(0, 1), :]).astype(BF16)
        ready_ref[part, :] = ready
        left = project(ready, 0) * jax.nn.sigmoid(project(ready, 1))
        left_all[chip, part, :] = left.astype(BF16)

    in_chunks(left_chunk)
    pl.semaphore_wait(barrier, chips - 1 + 2 * norths - 1)

    left_copies = []
    for step in reversed(range(chips - 1)):
        copy = pltpu.make_async_remote_copy(
            src_ref=left_all.at[chip],
            dst_ref=left_all.at[chip],
            send_sem=left_send_sem.at[step],
            recv_sem=left_recv_sem.at[chip],
            device_id=(north, order[step] * 2 + core),
            device_id_type=MESH,
        )
        copy.start()
        left_copies.append(copy)

    loads[4].wait()
    loads[5].wait()

    def right_chunk(part):
        ready = ready_ref[part, :]
        right = project(ready, 2) * jax.nn.sigmoid(project(ready, 3))
        right = right.astype(BF16)
        right_own[part, :] = right
        rows32[part, :] = right.astype(F32)

    in_chunks(right_chunk)
    right_copy = pltpu.make_async_remote_copy(
        src_ref=right_own,
        dst_ref=right_partner,
        send_sem=right_sem.at[0],
        recv_sem=right_sem.at[1],
        device_id=(north, partner),
        device_id_type=MESH,
    )
    right_copy.start()
    for line in range(lines):
        right32[line, pl.ds(0, columns), :] = rows32[pl.ds(line, columns, stride=lines), :]

    loads[6].wait()

    def gate_chunk(part):
        gate_ref[part, :] = jax.nn.sigmoid(project(ready_ref[part, :], 4))

    in_chunks(gate_chunk)

    right_copy.wait()
    rows32[...] = right_partner[...].astype(F32)
    for line in range(lines):
        right32[line, pl.ds(columns, columns), :] = rows32[pl.ds(line, columns, stride=lines), :]

    tiles = 2 * columns // LANES
    group = max(g for g in range(1, columns + 1) if columns % g == 0 and (g * tiles <= 36 or g == 1))

    def partial_sums(which):
        left32[...] = left_all[which].astype(F32)
        for first in range(0, columns, group):

            def term(line, totals):
                rights = [right32[line, pl.ds(LANES * t, LANES), :] for t in range(tiles)]
                new = []
                for i in range(group):
                    row = left32[pl.ds((first + i) * lines + line, LANES, stride=0), :]
                    for t in range(tiles):
                        new.append(totals[i * tiles + t] + row * rights[t])
                return tuple(new)

            zero = jnp.zeros((LANES, width), F32)
            totals = lax.fori_loop(0, lines, term, (zero,) * (group * tiles))
            for i in range(group):
                for t in range(tiles):
                    at = (first + i) * 2 * columns + LANES * t
                    sums32[pl.ds(at, LANES), :] = totals[i * tiles + t]
        for half in range(2):
            for j in range(columns):
                sums_dense[half, pl.ds(j * columns, columns), :] = sums32[
                    pl.ds(half * columns + j, columns, stride=2 * columns), :
                ]

    def sums_copy(step, half, owner, block):
        return pltpu.make_async_remote_copy(
            src_ref=sums_send.at[step, half],
            dst_ref=sums_all.at[north, block],
            send_sem=sums_send_sem.at[step, half],
            recv_sem=sums_recv_sem.at[north, block],
            device_id=(owner, partner if half else east),
            device_id_type=MESH,
        )

    sent = []
    for step in range(chips):
        source = chip if step == 0 else order[step - 1]
        if step:
            pltpu.make_async_remote_copy(
                src_ref=left_all.at[source],
                dst_ref=left_all.at[source],
                send_sem=left_send_sem.at[step - 1],
                recv_sem=left_recv_sem.at[source],
                device_id=(north, source * 2 + core),
                device_id_type=MESH,
            ).wait_recv()
        partial_sums(source)
        owner = (source * 2 + core) // ratio
        block = (source * 2 + core) % ratio
        sums_send[step, 1] = sums_dense[1].astype(BF16)
        sums_copy(step, 1, owner, block).start()
        here = owner == north

        @pl.when(here)
        def _():
            sums_all[north, block] = sums_dense[0].astype(BF16)

        @pl.when(jnp.logical_not(here))
        def _():
            sums_send[step, 0] = sums_dense[0].astype(BF16)
            sums_copy(step, 0, owner, block).start()

        sent.append((owner, block, here))

    for copy in left_copies:
        copy.wait_send()
    for step, (owner, block, here) in enumerate(sent):
        sums_copy(step, 1, owner, block).wait_send()

        @pl.when(jnp.logical_not(here))
        def _():
            sums_copy(step, 0, owner, block).wait_send()

    loads[7].wait()
    loads[8].wait()
    for block in range(ratio):
        for ahead in range(norths):
            origin = lax.rem(north + ahead, norths)
            arrival = pltpu.make_async_remote_copy(
                src_ref=sums_send.at[0, 0],
                dst_ref=sums_all.at[origin, block],
                send_sem=sums_send_sem.at[0, 0],
                recv_sem=sums_recv_sem.at[origin, block],
                device_id=(origin, partner),
                device_id_type=MESH,
            )
            if ahead:
                arrival.wait_recv()
            else:

                @pl.when(core != block % 2)
                def _():
                    arrival.wait_recv()

        total = sums_all[0, block].astype(F32)
        for origin in range(1, norths):
            total = total + sums_all[origin, block].astype(F32)
        sums32[pl.ds(0, piece), :] = total
        for j in range(columns):
            rows32[pl.ds(j * lines + block * columns, columns), :] = sums32[
                pl.ds(j * columns, columns), :
            ]

    def out_chunk(part):
        mixed = (rows32[part, :] * (lines * norths) ** (-0.5)).astype(BF16).astype(F32)
        scaled = scale_channels(mixed, gains[pl.ds(8, 1), :]).astype(BF16)
        out_ref[part, :] = (project(scaled, 5) * gate_ref[part, :]).astype(BF16)

    in_chunks(out_chunk)


def body(pair_rows, in_gain, left_weight, right_weight, left_gate, right_gate, mid_gain, out_weight, out_gate):
    lines, columns, width = pair_rows.shape
    norths, easts = lax.axis_size("north"), lax.axis_size("east")
    rows = lines * columns
    chips, ratio, piece = easts // 2, lines // columns, columns * columns
    dma = pltpu.SemaphoreType.DMA
    out = pl.pallas_call(
        functools.partial(kernel, norths, easts, lines, columns),
        out_shape=jax.ShapeDtypeStruct((rows, width), BF16),
        in_specs=[pl.BlockSpec(memory_space=pl.ANY)] * 9,
        out_specs=pl.BlockSpec(memory_space=pltpu.VMEM),
        scratch_shapes=[
            pltpu.VMEM((rows, width), BF16),
            pltpu.VMEM((16, width), F32),
            pltpu.VMEM((6, width, width), BF16),
            pltpu.VMEM((rows, width), F32),
            pltpu.VMEM((rows, width), BF16),
            pltpu.VMEM((rows, width), F32),
            pltpu.VMEM((chips, rows, width), BF16),
            pltpu.VMEM((rows, width), F32),
            pltpu.VMEM((rows, width), BF16),
            pltpu.VMEM((rows, width), BF16),
            pltpu.VMEM((lines, 2 * columns, width), F32),
            pltpu.VMEM((columns * 2 * columns, width), F32),
            pltpu.VMEM((2, piece, width), F32),
            pltpu.VMEM((chips, 2, piece, width), BF16),
            pltpu.VMEM((norths, ratio, piece, width), BF16),
            dma((9,)),
            dma((chips - 1,)),
            dma((chips,)),
            dma((2,)),
            dma((chips, 2)),
            dma((norths, ratio)),
        ],
        compiler_params=pltpu.CompilerParams(collective_id=0, has_side_effects=True),
        name="triangle",
    )(
        pair_rows.transpose(1, 0, 2).reshape(rows, width),
        in_gain.reshape(1, -1),
        left_weight,
        right_weight,
        left_gate,
        right_gate,
        mid_gain.reshape(1, -1),
        out_weight,
        out_gate,
    )
    return out.reshape(columns, lines, width).transpose(1, 0, 2)


def solution(mesh):
    placed = (P("north", "east", None), P(), P(), P(), P(), P(), P(), P(), P())
    return jax.shard_map(
        body, mesh=mesh, in_specs=placed, out_specs=P("north", "east", None), check_vma=False
    )
```

time: 54.5 us -> 19.3 us (0.35)
  blocking collectives: 23.7 us -> 0 us
  Pallas kernels: 0 us -> 17.4 us
  local copies, waits for them, and re-layouts: 11 us -> 1.52 us
  starting transfers between devices: 8.61 us -> 0 us
  waiting for transfers between devices: 6 us -> 0 us
  matrix products: 2.22 us -> 0 us
  other arithmetic: 1.94 us -> 0 us
    pallas_call x0 -> x1, Pallas kernels: none -> 17.4 us  [body(): pl.pallas_call(functools.partial(kernel, norths, easts, lines, columns),...]
    all_gather x1 -> x0, blocking collectives: 16.5 us -> none  [body(): lax.all_gather(left_lines, 'east', axis=1, tiled=True)]
    all_to_all x2 -> x0, starting transfers between devices: 8.61 us -> none  [the longest x1 5.32 us: body(): lax.all_to_all(right, 'north', split_axis=2, concat_axis=0, tiled=True)]
    all_to_all x1 -> x0, blocking collectives: 7.23 us -> none  [body(): lax.all_to_all(strip, 'north', split_axis=0, concat_axis=2, tiled=True)]
    all_to_all x2 -> x0, waiting for transfers between devices: 6 us -> none  [the longest x1 3.68 us: body(): lax.all_to_all(left, 'north', split_axis=2, concat_axis=0, tiled=True)]
    unnamed x24 -> x1, local copies, waits for them, and re-layouts: 7.43 us -> 1.52 us
    dot_general x7 -> x0, matrix products: 2.22 us -> none  [the longest x1 0.83 us: to_pair(): jnp.einsum('ijc,cd->ijd', ready, out_gate, preferred_element_type=jnp.flo...]
    convert_element_type x6 -> x0, local copies, waits for them, and re-layouts: 2.19 us -> none  [the longest x3 0.95 us: to_pair(): mixed.astype(jnp.float32)]
  transfers between devices with their start and end apart: 2 -> 0, of which waited for: 2 -> 0; matrix products, arithmetic and copies ran while one was open for 5% -> 0% of each run, Pallas kernels for 0% -> 0%
where the time goes in v1:
time: 19.3 us; the launch traced here: 19 us
  Pallas kernels  17.4 us (90%)
  local copies, waits for them, and re-layouts  1.52 us (8%)
    pallas_call x1, Pallas kernels, body(): pl.pallas_call(functools.partial(kernel, norths, easts, lines, columns),...  17.4 us
    unnamed x1, local copies, waits for them, and re-layouts  1.52 us

profile of v1, /device:TPU:0, one launch (start us, length us, event | category | flops | bytes accessed | tf_op | source)
XLA Modules:
  0.0 19.0 jit_solution(10470356024755262746)
XLA Ops:
  0.0 17.4 %triangle.1 = bf16[288,128]{1,0:T(8,128)(2,1)} custom-call(bf16[288,128]{1,0:T(8,128)(2,1)} %bitcast.9, f32[1,128]{1,0:T(1,128)} %bitcast.10, bf16[128,128]{1,0:T(8,128)(2,1)} %left_weight_hbm.1, bf16[128,128]{1,0:T(8,128)(2,1)} %right_weight_hbm.1, bf16[128,128]{1,0:T(8,128)(2,1)} %left_gate_hbm.1, bf16[128,128]{1,0:T(8,128)(2,1)} %right_gate_hbm.1, ...), custom_call_target="tpu_custom_call" | custom-call | tf_op jit(solution)/shard_map/triangle/pallas_call | solution.py:315
  17.4 1.5 %copy.11 = bf16[24,12,128]{2,0,1:T(8,128)(2,1)} copy(bf16[24,12,128]{2,0,1:T(8,128)(2,1)} %bitcast.8) | data formatting | bytes 147456

commit v2 on v1

v2 whole, which is shorter than its diff:
```python
import functools

import jax
import jax.numpy as jnp
from jax import lax
from jax.experimental import pallas as pl
from jax.experimental.pallas import tpu as pltpu
from jax.sharding import PartitionSpec as P

MESH = pl.DeviceIdType.MESH
F32 = jnp.float32
BF16 = jnp.bfloat16
LANES = 8


def scale_channels(values, channel_gain):
    centred = values - jnp.mean(values, axis=-1, keepdims=True)
    return (
        centred
        * lax.rsqrt(jnp.mean(centred * centred, axis=-1, keepdims=True) + 1e-05)
        * channel_gain
    )


def pieces_of(lines, columns):
    for pieces in (1,):
        if columns % pieces == 0 and all(
            columns // pieces * side % 16 == 0 for side in (lines, columns)
        ):
            return pieces
    return 1


def kernel(
    norths,
    easts,
    lines,
    columns,
    pair_hbm,
    in_gain_hbm,
    left_weight_hbm,
    right_weight_hbm,
    left_gate_hbm,
    right_gate_hbm,
    mid_gain_hbm,
    out_weight_hbm,
    out_gate_hbm,
    out_ref,
    pair_in,
    gains,
    weights,
    rows32,
    ready_ref,
    gate_ref,
    left_all,
    left32,
    right_own,
    right_partner,
    right32,
    sums32,
    sums_dense,
    sums_send,
    sums_all,
    load_sem,
    left_send_sem,
    left_recv_sem,
    right_sem,
    sums_send_sem,
    sums_recv_sem,
):
    rows, width = pair_in.shape
    chips = easts // 2
    ratio = lines // columns
    pieces = pieces_of(lines, columns)
    deep = columns // pieces
    left_rows, sum_rows = deep * lines, deep * columns

    north = lax.axis_index("north")
    east = lax.axis_index("east")
    chip = east // 2
    core = east % 2
    partner = chip * 2 + 1 - core

    loads = [
        (pair_hbm, pair_in),
        (in_gain_hbm, gains.at[pl.ds(0, 1)]),
        (left_weight_hbm, weights.at[0]),
        (left_gate_hbm, weights.at[1]),
        (right_weight_hbm, weights.at[2]),
        (right_gate_hbm, weights.at[3]),
        (out_gate_hbm, weights.at[4]),
        (out_weight_hbm, weights.at[5]),
        (mid_gain_hbm, gains.at[pl.ds(8, 1)]),
    ]
    loads = [
        pltpu.make_async_copy(source, target, load_sem.at[at])
        for at, (source, target) in enumerate(loads)
    ]
    for load in loads:
        load.start()

    barrier = pltpu.get_barrier_semaphore()
    routes = [(up, far) for far in (2, 1) for up in range(2)]

    def reached(up, far):
        return chip + far if up else chip - far

    def exists(up, far):
        return reached(up, far) < chips if up else reached(up, far) >= 0

    for up, far in routes:

        @pl.when(exists(up, far))
        def _():
            pl.semaphore_signal(
                barrier,
                inc=1,
                device_id=(north, reached(up, far) * 2 + core),
                device_id_type=MESH,
            )

    for step in range(norths):
        there = lax.rem(north + step, norths)
        if step:
            pl.semaphore_signal(barrier, inc=1, device_id=(there, east), device_id_type=MESH)
        pl.semaphore_signal(barrier, inc=1, device_id=(there, partner), device_id_type=MESH)

    loads[0].wait()
    loads[1].wait()

    chunk = rows // max(1, rows // 288)
    if rows % chunk or chunk % 16:
        chunk = rows

    def in_chunks(step):
        if chunk == rows:
            step(pl.ds(0, rows))
        else:

            @pl.loop(0, rows // chunk)
            def _(at):
                step(pl.ds(pl.multiple_of(at * chunk, chunk), chunk))

    def project(ready, which):
        return jnp.dot(ready, weights[which], preferred_element_type=F32)

    loads[2].wait()
    loads[3].wait()

    def left_copy(up, far, source, at):
        part = pl.ds(pl.multiple_of(at * left_rows, 16), left_rows)
        return pltpu.make_async_remote_copy(
            src_ref=left_all.at[source, part],
            dst_ref=left_all.at[source, part],
            send_sem=left_send_sem.at[up, far - 1, source, at],
            recv_sem=left_recv_sem.at[source, at],
            device_id=(north, reached(up, far) * 2 + core),
            device_id_type=MESH,
        )

    for at in range(pieces):
        part = pl.ds(at * left_rows, left_rows)
        ready = scale_channels(pair_in[part, :].astype(F32), gains[pl.ds(0, 1), :]).astype(BF16)
        ready_ref[part, :] = ready
        left = project(ready, 0) * jax.nn.sigmoid(project(ready, 1))
        left_all[chip, part, :] = left.astype(BF16)
        if at == 0:
            expected = sum(exists(*route).astype(jnp.int32) for route in routes)
            pl.semaphore_wait(barrier, expected + 2 * norths - 1)
        for up, far in routes:

            @pl.when(exists(up, far))
            def _():
                left_copy(up, far, chip, at).start()

    loads[4].wait()
    loads[5].wait()

    def right_chunk(part):
        ready = ready_ref[part, :]
        right = project(ready, 2) * jax.nn.sigmoid(project(ready, 3))
        right = right.astype(BF16)
        right_own[part, :] = right
        rows32[part, :] = right.astype(F32)

    in_chunks(right_chunk)
    right_copy = pltpu.make_async_remote_copy(
        src_ref=right_own,
        dst_ref=right_partner,
        send_sem=right_sem.at[0],
        recv_sem=right_sem.at[1],
        device_id=(north, partner),
        device_id_type=MESH,
    )
    right_copy.start()
    for line in range(lines):
        right32[line, pl.ds(0, columns), :] = rows32[pl.ds(line, columns, stride=lines), :]

    loads[6].wait()

    def gate_chunk(part):
        gate_ref[part, :] = jax.nn.sigmoid(project(ready_ref[part, :], 4))

    in_chunks(gate_chunk)

    right_copy.wait()
    rows32[...] = right_partner[...].astype(F32)
    for line in range(lines):
        right32[line, pl.ds(columns, columns), :] = rows32[pl.ds(line, columns, stride=lines), :]

    tiles = 2 * columns // LANES
    group = max(g for g in range(1, deep + 1) if deep % g == 0 and (g * tiles <= 36 or g == 1))

    def sums_copy(half, source, at):
        index = source * 2 + core
        return pltpu.make_async_remote_copy(
            src_ref=sums_send.at[source, half, at],
            dst_ref=sums_all.at[north, index % ratio, at],
            send_sem=sums_send_sem.at[source, half, at],
            recv_sem=sums_recv_sem.at[north, index % ratio, at],
            device_id=(index // ratio, partner if half else east),
            device_id_type=MESH,
        )

    def owned(source):
        return (source * 2 + core) // ratio == north

    def partial_sums(source, at):
        left32[...] = left_all[
            source, pl.ds(pl.multiple_of(at * left_rows, 16), left_rows), :
        ].astype(F32)
        for first in range(0, deep, group):

            def term(line, totals):
                rights = [right32[line, pl.ds(LANES * t, LANES), :] for t in range(tiles)]
                new = []
                for i in range(group):
                    row = left32[pl.ds((first + i) * lines + line, LANES, stride=0), :]
                    for t in range(tiles):
                        new.append(totals[i * tiles + t] + row * rights[t])
                return tuple(new)

            zero = jnp.zeros((LANES, width), F32)
            totals = lax.fori_loop(0, lines, term, (zero,) * (group * tiles), unroll=4)
            for i in range(group):
                for t in range(tiles):
                    row = (first + i) * 2 * columns + LANES * t
                    sums32[pl.ds(row, LANES), :] = totals[i * tiles + t]
        for half in range(2):
            for i in range(deep):
                sums_dense[half, pl.ds(i * columns, columns), :] = sums32[
                    pl.ds((2 * i + half) * columns, columns), :
                ]
        sums_send[source, 1, at] = sums_dense[1].astype(BF16)
        sums_copy(1, source, at).start()
        here = owned(source)

        @pl.when(here)
        def _():
            sums_all[north, (source * 2 + core) % ratio, at] = sums_dense[0].astype(BF16)

        @pl.when(jnp.logical_not(here))
        def _():
            sums_send[source, 0, at] = sums_dense[0].astype(BF16)
            sums_copy(0, source, at).start()

    @pl.loop(0, pieces)
    def _(at):
        partial_sums(chip, at)

    @pl.loop(0, chips // 2 * 2)
    def _(turn):
        hop = turn + 2 - 2 * (turn % 2)

        @pl.loop(0, pieces)
        def _(at):
            for up in range(2):
                source = chip - hop if up else chip + hop

                @pl.when(source >= 0 if up else source < chips)
                def _():
                    left_copy(up, 1, source, at).wait_recv()
                    for far in (2, 1):

                        @pl.when(jnp.logical_and(hop % 2 == 0, exists(up, far)))
                        def _():
                            left_copy(up, far, source, at).start()

                    partial_sums(source, at)

    @pl.loop(0, chips)
    def _(source):
        for at in range(pieces):
            for up, far in routes:
                hop = chip - source if up else source - chip
                passed = jnp.logical_and(hop >= 0, hop % 2 == 0)

                @pl.when(jnp.logical_and(passed, exists(up, far)))
                def _():
                    left_copy(up, far, source, at).wait_send()

            sums_copy(1, source, at).wait_send()

            @pl.when(jnp.logical_not(owned(source)))
            def _():
                sums_copy(0, source, at).wait_send()

    loads[7].wait()
    loads[8].wait()
    for block in range(ratio):
        for at in range(pieces):
            for ahead in range(norths):
                origin = lax.rem(north + ahead, norths)
                arrival = pltpu.make_async_remote_copy(
                    src_ref=sums_send.at[0, 0, at],
                    dst_ref=sums_all.at[origin, block, at],
                    send_sem=sums_send_sem.at[0, 0, at],
                    recv_sem=sums_recv_sem.at[origin, block, at],
                    device_id=(origin, partner),
                    device_id_type=MESH,
                )
                if ahead:
                    arrival.wait_recv()
                else:

                    @pl.when(core != block % 2)
                    def _():
                        arrival.wait_recv()

            total = sums_all[0, block, at].astype(F32)
            for origin in range(1, norths):
                total = total + sums_all[origin, block, at].astype(F32)
            sums32[pl.ds(0, sum_rows), :] = total
            for i in range(deep):
                first = block * columns + at * deep + i
                rows32[pl.ds(first, columns, stride=lines), :] = sums32[
                    pl.ds(i * columns, columns), :
                ]

    def out_chunk(part):
        mixed = (rows32[part, :] * (lines * norths) ** (-0.5)).astype(BF16).astype(F32)
        scaled = scale_channels(mixed, gains[pl.ds(8, 1), :]).astype(BF16)
        out_ref[part, :] = (project(scaled, 5) * gate_ref[part, :]).astype(BF16)

    in_chunks(out_chunk)


def body(pair_rows, in_gain, left_weight, right_weight, left_gate, right_gate, mid_gain, out_weight, out_gate):
    lines, columns, width = pair_rows.shape
    norths, easts = lax.axis_size("north"), lax.axis_size("east")
    rows = lines * columns
    chips, ratio = easts // 2, lines // columns
    pieces = pieces_of(lines, columns)
    left_rows, sum_rows = rows // pieces, columns * columns // pieces
    dma = pltpu.SemaphoreType.DMA
    out = pl.pallas_call(
        functools.partial(kernel, norths, easts, lines, columns),
        out_shape=pltpu.VMEM((rows, width), BF16),
        in_specs=[pl.BlockSpec(memory_space=pl.ANY)] * 9,
        out_specs=pl.BlockSpec(memory_space=pltpu.VMEM),
        scratch_shapes=[
            pltpu.VMEM((rows, width), BF16),
            pltpu.VMEM((16, width), F32),
            pltpu.VMEM((6, width, width), BF16),
            pltpu.VMEM((rows, width), F32),
            pltpu.VMEM((rows, width), BF16),
            pltpu.VMEM((rows, width), F32),
            pltpu.VMEM((chips, rows, width), BF16),
            pltpu.VMEM((left_rows, width), F32),
            pltpu.VMEM((rows, width), BF16),
            pltpu.VMEM((rows, width), BF16),
            pltpu.VMEM((lines, 2 * columns, width), F32),
            pltpu.VMEM((2 * sum_rows, width), F32),
            pltpu.VMEM((2, sum_rows, width), F32),
            pltpu.VMEM((chips, 2, pieces, sum_rows, width), BF16),
            pltpu.VMEM((norths, ratio, pieces, sum_rows, width), BF16),
            dma((9,)),
            dma((2, 2, chips, pieces)),
            dma((chips, pieces)),
            dma((2,)),
            dma((chips, 2, pieces)),
            dma((norths, ratio, pieces)),
        ],
        compiler_params=pltpu.CompilerParams(collective_id=0, has_side_effects=True),
        name="triangle",
    )(
        pair_rows.transpose(1, 0, 2).reshape(rows, width),
        in_gain.reshape(1, -1),
        left_weight,
        right_weight,
        left_gate,
        right_gate,
        mid_gain.reshape(1, -1),
        out_weight,
        out_gate,
    )
    return out.reshape(columns, lines, width).transpose(1, 0, 2)


def solution(mesh):
    placed = (P("north", "east", None), P(), P(), P(), P(), P(), P(), P(), P())
    return jax.shard_map(
        body, mesh=mesh, in_specs=placed, out_specs=P("north", "east", None), check_vma=False
    )
```

time: 19.3 us -> 17.5 us (0.907); the launches traced: 19 us -> 17.4 us
  local copies, waits for them, and re-layouts: 1.52 us -> 0.64 us
  Pallas kernels: 17.4 us -> 16.8 us
    unnamed x1, local copies, waits for them, and re-layouts: 1.52 us -> 0.64 us
    pallas_call x1, Pallas kernels: 17.4 us -> 16.8 us  [body(): pl.pallas_call(functools.partial(kernel, norths, easts, lines, columns),...]
where the time goes in v2:
time: 17.5 us; the launch traced here: 17.4 us
  Pallas kernels  16.8 us (96%)
  local copies, waits for them, and re-layouts  0.64 us (4%)
    pallas_call x1, Pallas kernels, body(): pl.pallas_call(functools.partial(kernel, norths, easts, lines, columns),...  16.8 us
    unnamed x1, local copies, waits for them, and re-layouts  0.64 us

profile of v2, /device:TPU:0, one launch (start us, length us, event | category | flops | bytes accessed | tf_op | source)
XLA Modules:
  0.0 17.4 jit_solution(7763482849838888381)
XLA Ops:
  0.0 16.8 %triangle.1 = bf16[288,128]{1,0:T(8,128)(2,1)S(1)} custom-call(bf16[288,128]{1,0:T(8,128)(2,1)} %bitcast.9, f32[1,128]{1,0:T(1,128)} %bitcast.10, bf16[128,128]{1,0:T(8,128)(2,1)} %left_weight_hbm.1, bf16[128,128]{1,0:T(8,128)(2,1)} %right_weight_hbm.1, bf16[128,128]{1,0:T(8,128)(2,1)} %left_gate_hbm.1, bf16[128,128]{1,0:T(8,128)(2,1)} %right_gate_hbm.1, ...), custom_call_target="tpu_custom_call" | custom-call | tf_op jit(solution)/shard_map/triangle/pallas_call | solution.py:356
  16.8 0.6 %copy.11 = bf16[24,12,128]{2,0,1:T(8,128)(2,1)} copy(bf16[24,12,128]{2,0,1:T(8,128)(2,1)S(1)} %bitcast.8) | data formatting | bytes 147456

commit v3 on v2

--- a/solution.py
+++ b/solution.py
@@ -268,9 +268,57 @@
     def _(at):
         partial_sums(chip, at)
 
+    loads[7].wait()
+    loads[8].wait()
+
+    def finish():
+        for block in range(ratio):
+            for at in range(pieces):
+                for ahead in range(norths):
+                    origin = lax.rem(north + ahead, norths)
+                    arrival = pltpu.make_async_remote_copy(
+                        src_ref=sums_send.at[0, 0, at],
+                        dst_ref=sums_all.at[origin, block, at],
+                        send_sem=sums_send_sem.at[0, 0, at],
+                        recv_sem=sums_recv_sem.at[origin, block, at],
+                        device_id=(origin, partner),
+                        device_id_type=MESH,
+                    )
+                    if ahead:
+                        arrival.wait_recv()
+                    else:
+
+                        @pl.when(core != block % 2)
+                        def _():
+                            arrival.wait_recv()
+
+                total = sums_all[0, block, at].astype(F32)
+                for origin in range(1, norths):
+                    total = total + sums_all[origin, block, at].astype(F32)
+                sums32[pl.ds(0, sum_rows), :] = total
+                for i in range(deep):
+                    first = block * columns + at * deep + i
+                    rows32[pl.ds(first, columns, stride=lines), :] = sums32[
+                        pl.ds(i * columns, columns), :
+                    ]
+
+        def out_chunk(part):
+            mixed = (rows32[part, :] * (lines * norths) ** (-0.5)).astype(BF16).astype(F32)
+            scaled = scale_channels(mixed, gains[pl.ds(8, 1), :]).astype(BF16)
+            out_ref[part, :] = (project(scaled, 5) * gate_ref[part, :]).astype(BF16)
+
+        in_chunks(out_chunk)
+
+    last = chips // 2 * 2
+    early = jnp.logical_and((north * ratio) // 2 == chip, ratio <= 2)
+
     @pl.loop(0, chips // 2 * 2)
     def _(turn):
         hop = turn + 2 - 2 * (turn % 2)
+
+        @pl.when(jnp.logical_and(early, turn == last - 1))
+        def _():
+            finish()
 
         @pl.loop(0, pieces)
         def _(at):
@@ -305,44 +353,9 @@
             def _():
                 sums_copy(0, source, at).wait_send()
 
-    loads[7].wait()
-    loads[8].wait()
-    for block in range(ratio):
-        for at in range(pieces):
-            for ahead in range(norths):
-                origin = lax.rem(north + ahead, norths)
-                arrival = pltpu.make_async_remote_copy(
-                    src_ref=sums_send.at[0, 0, at],
-                    dst_ref=sums_all.at[origin, block, at],
-                    send_sem=sums_send_sem.at[0, 0, at],
-                    recv_sem=sums_recv_sem.at[origin, block, at],
-                    device_id=(origin, partner),
-                    device_id_type=MESH,
-                )
-                if ahead:
-                    arrival.wait_recv()
-                else:
-
-                    @pl.when(core != block % 2)
-                    def _():
-                        arrival.wait_recv()
-
-            total = sums_all[0, block, at].astype(F32)
-            for origin in range(1, norths):
-                total = total + sums_all[origin, block, at].astype(F32)
-            sums32[pl.ds(0, sum_rows), :] = total
-            for i in range(deep):
-                first = block * columns + at * deep + i
-                rows32[pl.ds(first, columns, stride=lines), :] = sums32[
-                    pl.ds(i * columns, columns), :
-                ]
-
-    def out_chunk(part):
-        mixed = (rows32[part, :] * (lines * norths) ** (-0.5)).astype(BF16).astype(F32)
-        scaled = scale_channels(mixed, gains[pl.ds(8, 1), :]).astype(BF16)
-        out_ref[part, :] = (project(scaled, 5) * gate_ref[part, :]).astype(BF16)
-
-    in_chunks(out_chunk)
+    @pl.when(jnp.logical_not(early))
+    def _():
+        finish()
 
 
 def body(pair_rows, in_gain, left_weight, right_weight, left_gate, right_gate, mid_gain, out_weight, out_gate):

time: 17.5 us -> 17.1 us (0.977)
  Pallas kernels: 16.8 us -> 16.3 us
    pallas_call x1, Pallas kernels: 16.8 us -> 16.3 us  [body(): pl.pallas_call(functools.partial(kernel, norths, easts, lines, columns),...]
where the time goes in v3:
time: 17.1 us; the launch traced here: 17 us
  Pallas kernels  16.3 us (95%)
  local copies, waits for them, and re-layouts  0.64 us (4%)
    pallas_call x1, Pallas kernels, body(): pl.pallas_call(functools.partial(kernel, norths, easts, lines, columns),...  16.3 us
    unnamed x1, local copies, waits for them, and re-layouts  0.64 us

profile of v3, /device:TPU:0, one launch (start us, length us, event | category | flops | bytes accessed | tf_op | source)
XLA Modules:
  0.0 17.0 jit_solution(14948822273815173110)
XLA Ops:
  0.0 16.3 %triangle.1 = bf16[288,128]{1,0:T(8,128)(2,1)S(1)} custom-call(bf16[288,128]{1,0:T(8,128)(2,1)} %bitcast.9, f32[1,128]{1,0:T(1,128)} %bitcast.10, bf16[128,128]{1,0:T(8,128)(2,1)} %left_weight_hbm.1, bf16[128,128]{1,0:T(8,128)(2,1)} %right_weight_hbm.1, bf16[128,128]{1,0:T(8,128)(2,1)} %left_gate_hbm.1, bf16[128,128]{1,0:T(8,128)(2,1)} %right_gate_hbm.1, ...), custom_call_target="tpu_custom_call" | custom-call | tf_op jit(solution)/shard_map/triangle/pallas_call | solution.py:369
  16.4 0.6 %copy.11 = bf16[24,12,128]{2,0,1:T(8,128)(2,1)} copy(bf16[24,12,128]{2,0,1:T(8,128)(2,1)S(1)} %bitcast.8) | data formatting | bytes 147456
